TPU v7x, 32 devices: a 4x4x1 block of a 4x4x8 slice. The times are simulated.
32 devices in a mesh: dp: 1 (over z), cpo: 4 (over y), cpi: 8 (over x, core).
Axes of the slice: x: 4, y: 4, z: 1, core: 2. Of those that a mesh axis runs over, the one named last changes fastest.
The devices are a block of a 4x4x8 slice.
Arguments:
- hidden: bfloat16 [8192, 4096], P(('dp', 'cpo', 'cpi'))
- w_query: bfloat16 [4096, 32, 128], replicated
- w_key: bfloat16 [4096, 8, 128], replicated
- w_value: bfloat16 [4096, 8, 128], replicated
- w_out: bfloat16 [32, 128, 4096], replicated
Outputs:
- output: bfloat16 [8192, 4096], P(('dp', 'cpo', 'cpi'))
All inputs are finite; a program needn't handle non-finite values.
Results may differ from a plain program's by a relative error of at most 0.00596079.
Values are sent between devices in bfloat16 or wider.
A program may use at most 768 MiB of HBM per device.

v0:
```python
import jax
import jax.numpy as jnp
from jax import lax
from jax.sharding import PartitionSpec as P

ROPE_BASE = 500000.0
NEG_BIG = -1e30


def rope_tables(positions, head_dim):
    half_dim = head_dim // 2
    inv_freq = ROPE_BASE ** (-(2.0 / head_dim) * jnp.arange(half_dim, dtype=jnp.float32))
    angles = positions.astype(jnp.float32)[..., None] * inv_freq
    return jnp.cos(angles), jnp.sin(angles)


def apply_rope(proj_in, cos_b, sin_b):
    half_dim = proj_in.shape[-1] // 2
    lower_half = proj_in[..., :half_dim]
    upper_half = proj_in[..., half_dim:]
    return jnp.concatenate([lower_half * cos_b - upper_half * sin_b, upper_half * cos_b + lower_half * sin_b], axis=-1)


def softmax_update(state_in, q_blk, q_pos, keys_blk, values_blk, k_pos, score_scale):
    run_max, run_sum, acc_sum = state_in
    scores = jnp.einsum('qkgd,skd->qkgs', q_blk, keys_blk, preferred_element_type=jnp.float32) * score_scale
    causal = k_pos[None, None, None, :] <= q_pos[:, None, None, None]
    scores = jnp.where(causal, scores, -jnp.inf)
    new_max = jnp.maximum(run_max, scores.max(axis=-1))
    probs_blk = jnp.exp(scores - new_max[..., None])
    rescale = jnp.exp(run_max - new_max)
    new_sum = run_sum * rescale + probs_blk.sum(axis=-1)
    new_acc = acc_sum * rescale[..., None] + jnp.einsum('qkgs,skd->qkgd', probs_blk.astype(jnp.bfloat16), values_blk, preferred_element_type=jnp.float32)
    return new_max, new_sum, new_acc


def solution(mesh):
    n_outer = mesh.shape['cpo']
    n_inner = mesh.shape['cpi']
    n_dev = n_outer * n_inner
    shift_perm = [(idx, (idx + 1) % n_outer) for idx in range(n_outer)]

    def device_step(hidden, w_query, w_key, w_value, w_out):
        tok_rows, model_dim = hidden.shape
        chunk_len = tok_rows // 2
        q_heads = w_query.shape[1]
        head_dim = w_query.shape[2]
        kv_heads = w_key.shape[1]
        group_size = q_heads // kv_heads
        kv_loc = kv_heads // n_inner
        heads_loc = q_heads // n_inner
        block_len = n_inner * chunk_len
        score_scale = head_dim ** -0.5
        outer_idx = lax.axis_index('cpo')
        dev_rank = outer_idx * n_inner + lax.axis_index('cpi')
        offsets = jnp.arange(chunk_len, dtype=jnp.int32)
        local_pos = jnp.stack([dev_rank * chunk_len + offsets, (2 * n_dev - 1 - dev_rank) * chunk_len + offsets])
        cos_t, sin_t = rope_tables(local_pos, head_dim)
        cos_b = cos_t[:, :, None, :]
        sin_b = sin_t[:, :, None, :]
        x_halves = hidden.reshape(2, chunk_len, model_dim)
        q_proj = jnp.einsum('veo,ojf->vejf', x_halves, w_query, preferred_element_type=jnp.float32)
        k_proj = jnp.einsum('veo,ojf->vejf', x_halves, w_key, preferred_element_type=jnp.float32)
        v_proj = jnp.einsum('veo,ojf->vejf', x_halves, w_value, preferred_element_type=jnp.float32)
        queries = apply_rope(q_proj, cos_b, sin_b).astype(jnp.bfloat16)
        keys_loc = apply_rope(k_proj, cos_b, sin_b).astype(jnp.bfloat16)
        values_loc = v_proj.astype(jnp.bfloat16)

        def to_heads(tensor_in):
            tensor_in = tensor_in.reshape(2, 1, chunk_len, tensor_in.shape[2], head_dim)
            tensor_in = lax.all_to_all(tensor_in, 'cpi', 3, 1, tiled=True)
            return tensor_in.reshape(2, block_len, tensor_in.shape[3], head_dim)

        queries_h = to_heads(queries).reshape(2, block_len, kv_loc, group_size, head_dim)
        keys_h = to_heads(keys_loc)
        values_h = to_heads(values_loc)
        q_front = queries_h[0]
        q_back = queries_h[1]
        flat_idx = jnp.arange(block_len, dtype=jnp.int32)

        def block_positions(block_idx):
            front_pos = block_idx * block_len + flat_idx
            back_pos = (2 * n_dev - 1 - block_idx * n_inner - flat_idx // chunk_len) * chunk_len + flat_idx % chunk_len
            return front_pos, back_pos

        q_front_pos, q_back_pos = block_positions(outer_idx)

        def empty_state():
            stat_shape = (block_len, kv_loc, group_size)
            return (jnp.full(stat_shape, NEG_BIG, jnp.float32), jnp.zeros(stat_shape, jnp.float32), jnp.zeros(stat_shape + (head_dim,), jnp.float32))

        def attend_block(states, kv_block, src_idx):
            front_state, back_state = states
            keys_blk, values_blk = kv_block
            k_front_pos, k_back_pos = block_positions(src_idx)
            keys_front = keys_blk[0]
            values_front = values_blk[0]
            keys_both = keys_blk.reshape(2 * block_len, kv_loc, head_dim)
            values_both = values_blk.reshape(2 * block_len, kv_loc, head_dim)
            pos_both = jnp.concatenate([k_front_pos, k_back_pos])
            front_state = lax.cond(src_idx <= outer_idx, lambda state_in: softmax_update(state_in, q_front, q_front_pos, keys_front, values_front, k_front_pos, score_scale), lambda state_in: state_in, front_state)
            back_state = lax.cond(src_idx >= outer_idx, lambda state_in: softmax_update(state_in, q_back, q_back_pos, keys_both, values_both, pos_both, score_scale), lambda state_in: softmax_update(state_in, q_back, q_back_pos, keys_front, values_front, k_front_pos, score_scale), back_state)
            return front_state, back_state

        states = attend_block((empty_state(), empty_state()), (keys_h, values_h), outer_idx)

        def outer_step(step_idx, carry_in):
            states_in, kv_block = carry_in
            kv_block = lax.ppermute(kv_block, 'cpo', shift_perm)
            src_idx = (outer_idx - step_idx) % n_outer
            return attend_block(states_in, kv_block, src_idx), kv_block

        final_carry = lax.fori_loop(1, n_outer, outer_step, (states, (keys_h, values_h)))
        front_state, back_state = final_carry[0]
        out_front = (front_state[2] / front_state[1][..., None]).astype(jnp.bfloat16)
        out_back = (back_state[2] / back_state[1][..., None]).astype(jnp.bfloat16)
        out_heads = jnp.stack([out_front, out_back]).reshape(2, n_inner, chunk_len, heads_loc, head_dim)
        out_seq = lax.all_to_all(out_heads, 'cpi', 1, 3, tiled=True).reshape(tok_rows, q_heads, head_dim)
        result = jnp.einsum('thd,hdm->tm', out_seq, w_out, preferred_element_type=jnp.float32)
        return result.astype(jnp.bfloat16)

    row_spec = P(('dp', 'cpo', 'cpi'), None)
    weight_spec = P(None, None, None)
    return jax.shard_map(device_step, mesh=mesh, in_specs=(row_spec, weight_spec, weight_spec, weight_spec, weight_spec), out_specs=row_spec, check_vma=False)
```

profile of v0, /device:TPU:97, one launch (start us, length us, event | category | flops | bytes accessed | tf_op | source)
XLA Modules:
  0.0 496.2 jit_solution(9143281184101497721)
XLA Ops:
  0.0 12.0 %copy.67 = bf16[4096,8,128]{0,2,1:T(8,128)(2,1)} copy(bf16[4096,8,128]{2,1,0:T(8,128)(2,1)} %param.13) | data formatting | bytes 16777216 | tf_op args[2]
  24.2 42.7 %copy.70 = bf16[4096,32,128]{0,2,1:T(8,128)(2,1)} copy(bf16[4096,32,128]{2,1,0:T(8,128)(2,1)} %param.12) | data formatting | bytes 67108864 | tf_op args[1]
  66.9 15.9 %fusion.69 = f32[2,128,32,128]{1,3,2,0:T(8,128)} fusion(bf16[2,128,4096,1]{2,1,3,0:T(8,128)(2,1)S(1)} %bitcast.301, bf16[4096,32,128]{0,2,1:T(8,128)(2,1)} %copy.70), kind=kOutput, calls=%fused_computation.86 | convolution fusion | flops 8589934592 | bytes 39845888 | tf_op jit(solution)/shard_map/veo,ojf->vejf/dot_general | solution.py:62
  113.5 21.8 %all-to-all-done.1 = bf16[2,1,128,32,128]{2,4,0,1,3:T(8,128)(2,1)} async-done(((bf16[2,1,128,32,128]{2,4,0,1,3:T(8,128)(2,1)}), bf16[2,1,128,32,128]{2,4,0,1,3:T(8,128)(2,1)}, u32[]{:S(2)}, u32[]{:S(2)}) %all-to-all-start.1) | async-done | bytes 2097184 | tf_op jit(solution)/shard_map/all_to_all | solution.py:71
  158.5 15.2 %fusion.73 = (f32[1024,4]{0,1:T(4,128)S(1)}, f32[2048,1024,4]{1,0,2:T(8,128)}) fusion(pred[1024,2048]{0,1:T(8,128)(4,1)} %broadcast_compare_fusion.3, bf16[2048,128,1]{1,0,2:T(8,128)(2,1)} %bitcast.315, bf16[1024,4,128]{2,0,1:T(8,128)(2,1)S(1)} %bitcast.303), kind=kOutput, calls=%fused_computation.91 | convolution fusion | flops 2172645376 | bytes 37240832 | tf_op jit(solution)/shard_map/cond/branch_1_fun/qkgd,skd->qkgs/dot_general | solution.py:26
  173.7 14.4 %fusion.72 = f32[1024,4]{0,1:T(4,128)S(1)} fusion(f32[2048,1024,4]{1,0,2:T(8,128)} %get-tuple-element.896, f32[1024,4]{0,1:T(4,128)S(1)} %get-tuple-element.887, pred[1024,2048]{0,1:T(8,128)(4,1)S(1)} %copy-done.8), kind=kLoop, calls=%fused_computation.90 | loop fusion | flops 33550336 | bytes 35684352 | tf_op jit(solution)/shard_map/cond/branch_1_fun/reduce_sum | solution.py:32
  188.2 16.9 %fusion.91 = f32[1024,1,4,128]{0,3,2,1:T(8,128)} fusion(bf16[2048,128,1]{1,0,2:T(8,128)(2,1)S(1)} %bitcast.319, f32[2048,1024,4]{1,0,2:T(8,128)} %get-tuple-element.896, f32[1024,4]{0,1:T(4,128)S(1)} %get-tuple-element.887, pred[1024,2048]{0,1:T(8,128)(4,1)S(1)} %copy-done.8, f32[1024,4]{0,1:T(4,128)S(1)} %get-tuple-element.885), kind=kOutput, calls=%fused_computation.114 | convolution fusion | flops 2181562368 | bytes 38305792 | tf_op jit(solution)/shard_map/cond/branch_1_fun/qkgs,skd->qkgd/dot_general | solution.py:33
  208.0 235.9 %while.34 = (s32[]{:T(128)}, f32[1024,1,4]{0,2,1:T(4,128)S(1)}, f32[1024,1,4]{0,2,1:T(4,128)S(1)}, f32[1024,1,4,128]{3,0,2,1:T(8,128)}, f32[1024,1,4]{0,2,1:T(4,...) while((s32[]{:T(128)}, f32[1024,1,4]{0,2,1:T(4,128)S(1)}, ...), condition=%wide.region_15.16_spmd.clone.clone, body=%wide.region_4.15_spmd.clone.clone.sunk | while | flops 6586165248 | bytes 212923344 | solution.py:113
  236.0 49.4 %conditional.9 = (f32[1024,1,4]{0,2,1:T(4,128)}, f32[1024,1,4]{0,2,1:T(4,128)S(1)}, f32[1024,1,4,128]{3,0,2,1:T(8,128)}) conditional(s32[]{:T(128)} %convert_element_type.128, (s32[1024]{0:T(1024)S(1)}, s32[1024]{0:T(1024)S(1)}, bf16[1024,1,128]{2,0,1:T(8,128)(2,1)S(1)}, bf16[1024,1,4,128]{3,0,2,1:T(8,128)(2,1)S(1)}, f32[1024,1,4]{0,2,1:T(4,128)S(1)}, ...), branch_computations={%region_9.11_spmd, %region_12.14_spmd} | conditional | flops 4390400000 | bytes 119779408 | solution.py:102
  238.3 14.7 %fusion.44 = (f32[1024,4]{0,1:T(4,128)S(1)}, f32[2048,1024,4]{1,0,2:T(8,128)}) fusion(pred[1024,2048]{0,1:T(8,128)(4,1)S(1)} %broadcast_compare_fusion.2, bf16[2048,128,1]{1,0,2:T(8,128)(2,1)} %bitcast.305, bf16[1024,1,4,128]{3,0,2,1:T(8,128)(2,1)S(1)} %get-tuple-element.647), kind=kOutput, calls=%fused_computation.50 | convolution fusion | flops 2172645376 | bytes 37240832 | tf_op jit(solution)/shard_map/while/body/eval_jaxpr/cond/branch_1_fun/qkgd,skd->qkgs/dot_general | solution.py:26
  253.6 14.3 %fusion.43 = f32[1024,4]{0,1:T(4,128)S(1)} fusion(f32[2048,1024,4]{1,0,2:T(8,128)} %get-tuple-element.874, f32[1024,4]{0,1:T(4,128)} %bitcast.36, pred[1024,2048]{0,1:T(8,128)(4,1)S(1)} %broadcast_compare_fusion.2), kind=kLoop, calls=%fused_computation.49 | loop fusion | flops 33550336 | bytes 35684352 | tf_op jit(solution)/shard_map/while/body/eval_jaxpr/cond/branch_1_fun/reduce_sum | solution.py:32
  268.7 16.7 %bitcast_add_fusion.4 = f32[1024,1,4,128]{3,0,2,1:T(8,128)} fusion(f32[1024,1,4,128]{3,0,2,1:T(8,128)} %get-tuple-element.649, bf16[2048,128,1]{1,0,2:T(8,128)(2,1)} %bitcast.306, f32[2048,1024,4]{1,0,2:T(8,128)} %get-tuple-element.874, f32[1024,4]{0,1:T(4,128)} %bitcast.36, pred[1024,2048]{0,1:T(8,128)(4,1)S(1)} %broadcast_compare_fusion.2, ...), kind=kOutput, calls=%fused_computation.55 | convolution fusion | flops 2182086656 | bytes 40402944 | tf_op jit(solution)/shard_map/while/body/eval_jaxpr/cond/branch_1_fun/qkgs,skd->qkgd/dot_general | solution.py:33
  288.7 13.0 %collective-permute-done = bf16[2,1024,1,128]{3,1,0,2:T(8,128)(2,1)S(1)} collective-permute-done((bf16[2,1024,1,128]{3,1,0,2:T(8,128)(2,1)}, bf16[2,1024,1,128]{3,1,0,2:T(8,128)(2,1)S(1)}, u32[]{:S(2)}, u32[]{:S(2)}) %collective-permute-start) | collective-permute-done | bytes 524320 | tf_op jit(solution)/shard_map/while/body/eval_jaxpr/ppermute | solution.py:109
  313.9 49.4 %conditional.9 = (f32[1024,1,4]{0,2,1:T(4,128)}, f32[1024,1,4]{0,2,1:T(4,128)S(1)}, f32[1024,1,4,128]{3,0,2,1:T(8,128)}) conditional(s32[]{:T(128)} %convert_element_type.128, (s32[1024]{0:T(1024)S(1)}, s32[1024]{0:T(1024)S(1)}, bf16[1024,1,128]{2,0,1:T(8,128)(2,1)S(1)}, bf16[1024,1,4,128]{3,0,2,1:T(8,128)(2,1)S(1)}, f32[1024,1,4]{0,2,1:T(4,128)S(1)}, ...), branch_computations={%region_9.11_spmd, %region_12.14_spmd} | conditional | flops 4390400000 | bytes 119779408 | solution.py:102
  316.2 14.7 %fusion.44 = (f32[1024,4]{0,1:T(4,128)S(1)}, f32[2048,1024,4]{1,0,2:T(8,128)}) fusion(pred[1024,2048]{0,1:T(8,128)(4,1)S(1)} %broadcast_compare_fusion.2, bf16[2048,128,1]{1,0,2:T(8,128)(2,1)} %bitcast.305, bf16[1024,1,4,128]{3,0,2,1:T(8,128)(2,1)S(1)} %get-tuple-element.647), kind=kOutput, calls=%fused_computation.50 | convolution fusion | flops 2172645376 | bytes 37240832 | tf_op jit(solution)/shard_map/while/body/eval_jaxpr/cond/branch_1_fun/qkgd,skd->qkgs/dot_general | solution.py:26
  331.5 14.3 %fusion.43 = f32[1024,4]{0,1:T(4,128)S(1)} fusion(f32[2048,1024,4]{1,0,2:T(8,128)} %get-tuple-element.874, f32[1024,4]{0,1:T(4,128)} %bitcast.36, pred[1024,2048]{0,1:T(8,128)(4,1)S(1)} %broadcast_compare_fusion.2), kind=kLoop, calls=%fused_computation.49 | loop fusion | flops 33550336 | bytes 35684352 | tf_op jit(solution)/shard_map/while/body/eval_jaxpr/cond/branch_1_fun/reduce_sum | solution.py:32
  346.6 16.7 %bitcast_add_fusion.4 = f32[1024,1,4,128]{3,0,2,1:T(8,128)} fusion(f32[1024,1,4,128]{3,0,2,1:T(8,128)} %get-tuple-element.649, bf16[2048,128,1]{1,0,2:T(8,128)(2,1)} %bitcast.306, f32[2048,1024,4]{1,0,2:T(8,128)} %get-tuple-element.874, f32[1024,4]{0,1:T(4,128)} %bitcast.36, pred[1024,2048]{0,1:T(8,128)(4,1)S(1)} %broadcast_compare_fusion.2, ...), kind=kOutput, calls=%fused_computation.55 | convolution fusion | flops 2182086656 | bytes 40402944 | tf_op jit(solution)/shard_map/while/body/eval_jaxpr/cond/branch_1_fun/qkgs,skd->qkgd/dot_general | solution.py:33
  366.7 12.2 %collective-permute-done = bf16[2,1024,1,128]{3,1,0,2:T(8,128)(2,1)S(1)} collective-permute-done((bf16[2,1024,1,128]{3,1,0,2:T(8,128)(2,1)}, bf16[2,1024,1,128]{3,1,0,2:T(8,128)(2,1)S(1)}, u32[]{:S(2)}, u32[]{:S(2)}) %collective-permute-start) | collective-permute-done | bytes 524320 | tf_op jit(solution)/shard_map/while/body/eval_jaxpr/ppermute | solution.py:109
  390.9 49.4 %conditional.9 = (f32[1024,1,4]{0,2,1:T(4,128)}, f32[1024,1,4]{0,2,1:T(4,128)S(1)}, f32[1024,1,4,128]{3,0,2,1:T(8,128)}) conditional(s32[]{:T(128)} %convert_element_type.128, (s32[1024]{0:T(1024)S(1)}, s32[1024]{0:T(1024)S(1)}, bf16[1024,1,128]{2,0,1:T(8,128)(2,1)S(1)}, bf16[1024,1,4,128]{3,0,2,1:T(8,128)(2,1)S(1)}, f32[1024,1,4]{0,2,1:T(4,128)S(1)}, ...), branch_computations={%region_9.11_spmd, %region_12.14_spmd} | conditional | flops 4390400000 | bytes 119779408 | solution.py:102
  393.2 14.7 %fusion.44 = (f32[1024,4]{0,1:T(4,128)S(1)}, f32[2048,1024,4]{1,0,2:T(8,128)}) fusion(pred[1024,2048]{0,1:T(8,128)(4,1)S(1)} %broadcast_compare_fusion.2, bf16[2048,128,1]{1,0,2:T(8,128)(2,1)} %bitcast.305, bf16[1024,1,4,128]{3,0,2,1:T(8,128)(2,1)S(1)} %get-tuple-element.647), kind=kOutput, calls=%fused_computation.50 | convolution fusion | flops 2172645376 | bytes 37240832 | tf_op jit(solution)/shard_map/while/body/eval_jaxpr/cond/branch_1_fun/qkgd,skd->qkgs/dot_general | solution.py:26
  408.6 14.3 %fusion.43 = f32[1024,4]{0,1:T(4,128)S(1)} fusion(f32[2048,1024,4]{1,0,2:T(8,128)} %get-tuple-element.874, f32[1024,4]{0,1:T(4,128)} %bitcast.36, pred[1024,2048]{0,1:T(8,128)(4,1)S(1)} %broadcast_compare_fusion.2), kind=kLoop, calls=%fused_computation.49 | loop fusion | flops 33550336 | bytes 35684352 | tf_op jit(solution)/shard_map/while/body/eval_jaxpr/cond/branch_1_fun/reduce_sum | solution.py:32
  423.7 16.7 %bitcast_add_fusion.4 = f32[1024,1,4,128]{3,0,2,1:T(8,128)} fusion(f32[1024,1,4,128]{3,0,2,1:T(8,128)} %get-tuple-element.649, bf16[2048,128,1]{1,0,2:T(8,128)(2,1)} %bitcast.306, f32[2048,1024,4]{1,0,2:T(8,128)} %get-tuple-element.874, f32[1024,4]{0,1:T(4,128)} %bitcast.36, pred[1024,2048]{0,1:T(8,128)(4,1)S(1)} %broadcast_compare_fusion.2, ...), kind=kOutput, calls=%fused_computation.55 | convolution fusion | flops 2182086656 | bytes 40402944 | tf_op jit(solution)/shard_map/while/body/eval_jaxpr/cond/branch_1_fun/qkgs,skd->qkgd/dot_general | solution.py:33
  448.2 32.1 %all_to_all.60 = bf16[2,8,128,4,128]{4,2,0,3,1:T(8,128)(2,1)S(1)} all-to-all(bf16[2,8,128,4,128]{4,2,0,3,1:T(8,128)(2,1)S(1)} %copy.92), channel_id=1, replica_groups=mesh['dp'=1,'cpo'=4,'cpi'=8] {'cpi'}, dimensions={1} | all-to-all | bytes 4194304 | tf_op jit(solution)/shard_map/all_to_all | solution.py:118
  480.2 15.6 %fusion.90 = bf16[256,4096]{1,0:T(8,128)(2,1)} fusion(bf16[256,32,128]{2,0,1:T(8,128)(2,1)S(1)} %bitcast.313, bf16[32,128,4096]{2,1,0:T(8,128)(2,1)} %param.15), kind=kOutput, calls=%fused_computation.109 | convolution fusion | flops 8590983168 | bytes 37748736 | tf_op jit(solution)/shard_map/thd,hdm->tm/dot_general | solution.py:119
  (141 shorter events, 146.2 us)
Async XLA Ops:
  0.0 12.0 %copy-start = (bf16[256,4096]{1,0:T(8,128)(2,1)S(1)}, bf16[256,4096]{1,0:T(8,128)(2,1)}, u32[]{:S(2)}) copy-start(bf16[256,4096]{1,0:T(8,128)(2,1)} %param.11) | copy-start | bytes 6291460
  18.2 71.2 %all-to-all-start = ((bf16[2,1,128,8,128]{2,4,0,1,3:T(8,128)(2,1)}), bf16[2,1,128,8,128]{2,4,0,1,3:T(8,128)(2,1)S(1)}, u32[]{:S(2)}, u32[]{:S(2)}) async-start(bf16[2,1,128,8,128]{2,4,0,1,3:T(8,128)(2,1)} %copy.68), calls=%async_computation | async-start | bytes 1048576 | tf_op jit(solution)/shard_map/all_to_all | solution.py:71
  89.4 14.0 %all-to-all-start.2 = ((bf16[2,1,128,8,128]{4,2,0,1,3:T(8,128)(2,1)}), bf16[2,1,128,8,128]{4,2,0,1,3:T(8,128)(2,1)S(1)}, u32[]{:S(2)}, u32[]{:S(2)}) async-start(bf16[2,1,128,8,128]{4,2,0,1,3:T(8,128)(2,1)} %copy.74), calls=%async_computation.2 | async-start | bytes 1048576 | tf_op jit(solution)/shard_map/all_to_all | solution.py:71
  103.4 31.9 %all-to-all-start.1 = ((bf16[2,1,128,32,128]{2,4,0,1,3:T(8,128)(2,1)}), bf16[2,1,128,32,128]{2,4,0,1,3:T(8,128)(2,1)}, u32[]{:S(2)}, u32[]{:S(2)}) async-start(bf16[2,1,128,32,128]{2,4,0,1,3:T(8,128)(2,1)} %copy.71), calls=%async_computation.1 | async-start | bytes 4194304 | tf_op jit(solution)/shard_map/all_to_all | solution.py:71
  112.6 33.4 %copy-start.13 = (bf16[2,1,128,8,128]{4,2,3,0,1:T(8,128)(2,1)}, bf16[2,1,128,8,128]{4,2,3,0,1:T(8,128)(2,1)S(1)}, u32[]{:S(2)}) copy-start(bf16[2,1,128,8,128]{4,2,3,0,1:T(8,128)(2,1)S(1)} %copy.69) | copy-start | bytes 1572868
  112.6 33.3 %copy-start.14 = (bf16[2,1,128,8,128]{4,2,3,0,1:T(8,128)(2,1)}, bf16[2,1,128,8,128]{4,2,3,0,1:T(8,128)(2,1)S(1)}, u32[]{:S(2)}) copy-start(bf16[2,1,128,8,128]{4,2,3,0,1:T(8,128)(2,1)S(1)} %copy.103) | copy-start | bytes 1572868
  146.0 3.7 copy-start.16
  158.5 15.2 %copy-start.8 = (pred[1024,2048]{0,1:T(8,128)(4,1)S(1)}, pred[1024,2048]{0,1:T(8,128)(4,1)}, u32[]{:S(2)}) copy-start(pred[1024,2048]{0,1:T(8,128)(4,1)} %broadcast_compare_fusion.3) | copy-start | bytes 6291460
  173.7 14.4 %copy-start.15 = (bf16[2,1,128,8,128]{4,2,3,0,1:T(8,128)(2,1)S(1)}, bf16[2,1,128,8,128]{4,2,3,0,1:T(8,128)(2,1)}, u32[]{:S(2)}) copy-start(bf16[2,1,128,8,128]{4,2,3,0,1:T(8,128)(2,1)} %copy-done.14) | copy-start | bytes 1572868
  208.1 15.7 %collective-permute-start = (bf16[2,1024,1,128]{3,1,0,2:T(8,128)(2,1)}, bf16[2,1024,1,128]{3,1,0,2:T(8,128)(2,1)S(1)}, u32[]{:S(2)}, u32[]{:S(2)}) collective-permute-start(bf16[2,1024,1,128]{3,1,0,2:T(8,128)(2,1)} %get-tuple-element.1040), channel_id=1, source_target_pairs={{0,8},{8,16},{16,24},{24,0},{1,9},{9,17},{17,25},{25,1},{2,10},{10... | collective-permute-start | bytes 1572872 | tf_op jit(solution)/shard_map/while/body/eval_jaxpr/ppermute | solution.py:109
  210.1 25.0 %collective-permute-start.1 = (bf16[2,1024,1,128]{3,1,0,2:T(8,128)(2,1)}, bf16[2,1024,1,128]{3,1,0,2:T(8,128)(2,1)S(1)}, u32[]{:S(2)}, u32[]{:S(2)}) collective-permute-start(bf16[2,1024,1,128]{3,1,0,2:T(8,128)(2,1)} %get-tuple-element.1041), channel_id=1, source_target_pairs={{0,8},{8,16},{16,24},{24,0},{1,9},{9,17},{17,25},{25,1},{2,10},{10... | collective-permute-start | bytes 1572872 | tf_op jit(solution)/shard_map/while/body/eval_jaxpr/ppermute | solution.py:109
  223.8 12.0 %copy-start.2 = (bf16[2,1024,1,128]{3,1,0,2:T(8,128)(2,1)}, bf16[2,1024,1,128]{3,1,0,2:T(8,128)(2,1)S(1)}, u32[]{:S(2)}) copy-start(bf16[2,1024,1,128]{3,1,0,2:T(8,128)(2,1)S(1)} %collective-permute-done) | copy-start | bytes 1572868 | tf_op jit(solution)/shard_map/while
  286.1 1.0 copy-start.3
  286.1 1.8 copy-start.6
  288.7 13.1 %collective-permute-start = (bf16[2,1024,1,128]{3,1,0,2:T(8,128)(2,1)}, bf16[2,1024,1,128]{3,1,0,2:T(8,128)(2,1)S(1)}, u32[]{:S(2)}, u32[]{:S(2)}) collective-permute-start(bf16[2,1024,1,128]{3,1,0,2:T(8,128)(2,1)} %get-tuple-element.1040), channel_id=1, source_target_pairs={{0,8},{8,16},{16,24},{24,0},{1,9},{9,17},{17,25},{25,1},{2,10},{10... | collective-permute-start | bytes 1572872 | tf_op jit(solution)/shard_map/while/body/eval_jaxpr/ppermute | solution.py:109
  288.7 24.3 %collective-permute-start.1 = (bf16[2,1024,1,128]{3,1,0,2:T(8,128)(2,1)}, bf16[2,1024,1,128]{3,1,0,2:T(8,128)(2,1)S(1)}, u32[]{:S(2)}, u32[]{:S(2)}) collective-permute-start(bf16[2,1024,1,128]{3,1,0,2:T(8,128)(2,1)} %get-tuple-element.1041), channel_id=1, source_target_pairs={{0,8},{8,16},{16,24},{24,0},{1,9},{9,17},{17,25},{25,1},{2,10},{10... | collective-permute-start | bytes 1572872 | tf_op jit(solution)/shard_map/while/body/eval_jaxpr/ppermute | solution.py:109
  301.7 12.0 %copy-start.2 = (bf16[2,1024,1,128]{3,1,0,2:T(8,128)(2,1)}, bf16[2,1024,1,128]{3,1,0,2:T(8,128)(2,1)S(1)}, u32[]{:S(2)}) copy-start(bf16[2,1024,1,128]{3,1,0,2:T(8,128)(2,1)S(1)} %collective-permute-done) | copy-start | bytes 1572868 | tf_op jit(solution)/shard_map/while
  364.0 1.0 copy-start.3
  364.0 1.8 copy-start.6
  366.6 12.2 %collective-permute-start = (bf16[2,1024,1,128]{3,1,0,2:T(8,128)(2,1)}, bf16[2,1024,1,128]{3,1,0,2:T(8,128)(2,1)S(1)}, u32[]{:S(2)}, u32[]{:S(2)}) collective-permute-start(bf16[2,1024,1,128]{3,1,0,2:T(8,128)(2,1)} %get-tuple-element.1040), channel_id=1, source_target_pairs={{0,8},{8,16},{16,24},{24,0},{1,9},{9,17},{17,25},{25,1},{2,10},{10... | collective-permute-start | bytes 1572872 | tf_op jit(solution)/shard_map/while/body/eval_jaxpr/ppermute | solution.py:109
  366.6 23.4 %collective-permute-start.1 = (bf16[2,1024,1,128]{3,1,0,2:T(8,128)(2,1)}, bf16[2,1024,1,128]{3,1,0,2:T(8,128)(2,1)S(1)}, u32[]{:S(2)}, u32[]{:S(2)}) collective-permute-start(bf16[2,1024,1,128]{3,1,0,2:T(8,128)(2,1)} %get-tuple-element.1041), channel_id=1, source_target_pairs={{0,8},{8,16},{16,24},{24,0},{1,9},{9,17},{17,25},{25,1},{2,10},{10... | collective-permute-start | bytes 1572872 | tf_op jit(solution)/shard_map/while/body/eval_jaxpr/ppermute | solution.py:109
  378.8 12.0 %copy-start.2 = (bf16[2,1024,1,128]{3,1,0,2:T(8,128)(2,1)}, bf16[2,1024,1,128]{3,1,0,2:T(8,128)(2,1)S(1)}, u32[]{:S(2)}) copy-start(bf16[2,1024,1,128]{3,1,0,2:T(8,128)(2,1)S(1)} %collective-permute-done) | copy-start | bytes 1572868 | tf_op jit(solution)/shard_map/while
  441.0 1.8 copy-start.6
  480.2 15.6 %copy-start.1 = (bf16[256,4096]{1,0:T(8,128)(2,1)S(1)}, bf16[256,4096]{1,0:T(8,128)(2,1)}, u32[]{:S(2)}) copy-start(bf16[256,4096]{1,0:T(8,128)(2,1)} %param.11) | copy-start | bytes 6291460
  (10 other events, 9.2 us)
where the time goes:
time: 505 us; the launch traced here: 496 us
  matrix products  178 us (35%)
  waiting for transfers between devices  97 us (19%)
  local copies, waits for them, and re-layouts  87.5 us (17%)
  other arithmetic  79.9 us (16%)
  blocking collectives  32.1 us (6%)
  starting transfers between devices  20.4 us (4%)
    dot_general x5, matrix products, softmax_update(): jnp.einsum('qkgs,skd->qkgd', probs_blk.astype(jnp.bfloat16), values_blk,...  72.7 us
    ppermute x6, waiting for transfers between devices, outer_step(): kv_block = lax.ppermute(kv_block, 'cpo', shift_perm)  70.7 us
    dot_general x5, matrix products, softmax_update(): jnp.einsum('qkgd,skd->qkgs', q_blk, keys_blk, preferred_element_type=jnp....  63.4 us
    reduce_sum x5, other arithmetic, softmax_update(): new_sum = run_sum * rescale + probs_blk.sum(axis=-1)  61 us
    unnamed x18, local copies, waits for them, and re-layouts  60.6 us
    all_to_all x1, blocking collectives, device_step(): lax.all_to_all(out_heads, 'cpi', 1, 3, tiled=True)  32.1 us
    all_to_all x3, waiting for transfers between devices, to_heads(): tensor_in = lax.all_to_all(tensor_in, 'cpi', 3, 1, tiled=True)  26.3 us
    all_to_all x3, starting transfers between devices, to_heads(): tensor_in = lax.all_to_all(tensor_in, 'cpi', 3, 1, tiled=True)  16.6 us
  transfers between devices with their start and end apart: 9, of which 8 were waited for; matrix products, arithmetic and copies ran while one was open for 15% of the time, Pallas kernels for 0%

commit v1 on v0

v1 whole, which is shorter than its diff:
```python
import functools

import jax
import jax.numpy as jnp
from jax import lax
from jax.experimental import pallas as pl
from jax.experimental.pallas import tpu as pltpu
from jax.sharding import PartitionSpec as P

ROPE_BASE = 500000.0
NEG_BIG = -1e30
LOG2E = 1.4426950408889634
MESH = pl.DeviceIdType.MESH
F32 = jnp.float32
BF16 = jnp.bfloat16


def rope_tables(positions, head_dim):
    half_dim = head_dim // 2
    inv_freq = ROPE_BASE ** (-(2.0 / head_dim) * jnp.arange(half_dim, dtype=F32))
    angles = positions.astype(F32)[..., None] * inv_freq
    return jnp.cos(angles), jnp.sin(angles)


def layer_kernel(n_outer, n_inner, x_ref, cos_ref, sin_ref, wq_ref, wk_ref, wv_ref, wo_ref, out_ref,
                 qk_send, v_send, k_all, v_all, q_all, o_stage, o_all,
                 w_sem, send_k, recv_k, send_v, recv_v, send_q, recv_q, send_o, recv_o, send_y, recv_y):
    outer = lax.axis_index("cpo")
    inner = lax.axis_index("cpi")
    rows, model = x_ref.shape
    chunk = rows // 2
    hd = cos_ref.shape[1]
    block = n_inner * chunk
    n_blocks = 2 * n_outer
    groups = wq_ref.shape[1] // n_inner
    per_kv = groups
    tile = 2 * chunk
    n_tiles = block // tile
    cols = per_kv * tile
    scale = LOG2E * hd ** -0.5
    up = lax.rem(outer + 1, n_outer)
    down = lax.rem(outer + n_outer - 1, n_outer)
    far = lax.rem(outer + 2, n_outer)
    mirror = n_blocks - 1

    def across(peer):
        return {"cpi": peer}

    def along(peer):
        return {"cpo": peer}

    def landed(ref, sem):
        pltpu.make_async_copy(ref, ref, sem).wait()

    barrier = pltpu.get_barrier_semaphore()
    for d in range(1, n_inner):
        pl.semaphore_signal(barrier, inc=1, device_id=across(lax.rem(inner + d, n_inner)), device_id_type=MESH)
    for peer in (up, down):
        pl.semaphore_signal(barrier, inc=1, device_id=along(peer), device_id_type=MESH)

    def half_block(half, owner_outer):
        return owner_outer if half == 0 else mirror - owner_outer

    def half_rows(half, who):
        start = who * chunk if half == 0 else (n_inner - 1 - who) * chunk
        return pl.ds(pl.multiple_of(start, chunk), chunk)

    def k_copy(half, peer, owner, sem_peer):
        return dict(src_ref=qk_send.at[half, peer], dst_ref=k_all.at[half_block(half, outer), half_rows(half, owner), :])

    def v_copy(half, peer, owner):
        return dict(src_ref=v_send.at[half, peer], dst_ref=v_all.at[half_block(half, outer), :, half_rows(half, owner)])

    def q_copy(half, peer, owner):
        heads = pl.ds(n_inner + peer * per_kv, per_kv)
        return dict(src_ref=qk_send.at[half, heads], dst_ref=q_all.at[half, :, half_rows(half, owner), :])

    def exchange(make, send, recv, peer):
        @pl.when(peer != inner)
        def _():
            for half in range(2):
                refs = make(half, peer, inner)
                pltpu.make_async_remote_copy(send_sem=send.at[half, peer], recv_sem=recv.at[half, inner],
                                             device_id=across(peer), device_id_type=MESH, **refs).start()

        @pl.when(peer == inner)
        def _():
            for half in range(2):
                refs = make(half, peer, inner)
                pltpu.make_async_copy(refs["src_ref"], refs["dst_ref"], recv.at[half, inner]).start()

    def kv_landed():
        def one(src, _):
            for half in range(2):
                landed(k_all.at[half_block(half, outer), half_rows(half, src), :], recv_k.at[half, src])
                landed(v_all.at[half_block(half, outer), :, half_rows(half, src)], recv_v.at[half, src])
            return 0
        lax.fori_loop(0, n_inner, one, 0)

    def y_parts(src):
        return (k_all.at[src], k_all.at[mirror - src], v_all.at[src], v_all.at[mirror - src])

    def y_send(src, part, slot, lane, peer):
        ref = y_parts(src)[part]
        return pltpu.make_async_remote_copy(src_ref=ref, dst_ref=ref, send_sem=send_y.at[slot, part],
                                            recv_sem=recv_y.at[lane, part], device_id=along(peer), device_id_type=MESH)

    def project(w_buf, y_buf):
        def fetch(e, do):
            slot = lax.rem(e, 2)

            @pl.when(e == 0)
            def _():
                do(pltpu.make_async_copy(wk_ref, w_buf.at[slot], w_sem.at[slot]))

            @pl.when(e == 1)
            def _():
                do(pltpu.make_async_copy(wv_ref, w_buf.at[slot], w_sem.at[slot]))

            @pl.when(e >= 2)
            def _():
                heads = pl.ds(pl.multiple_of(group_of(e) * n_inner, n_inner), n_inner)
                do(pltpu.make_async_copy(wq_ref.at[:, heads, :], w_buf.at[slot], w_sem.at[slot]))

        def group_of(e):
            return lax.rem(inner * groups // n_inner + e, groups)

        fetch(0, lambda c: c.start())
        fetch(1, lambda c: c.start())
        pl.semaphore_wait(barrier, n_inner + 1)

        def step(e, _):
            slot = lax.rem(e, 2)
            fetch(e, lambda c: c.wait())
            y_buf[...] = jnp.dot(x_ref[...], w_buf[slot].reshape(model, n_inner * hd), preferred_element_type=F32)

            @pl.when(e + 2 < groups + 2)
            def _():
                fetch(e + 2, lambda c: c.start())

            @pl.when(e == 1)
            def _():
                for h in range(n_inner):
                    vt = y_buf[:, h * hd:(h + 1) * hd].T.astype(BF16)
                    for half in range(2):
                        v_send[half, h] = vt[:, half * chunk:(half + 1) * chunk]

                def one(d, _):
                    exchange(v_copy, send_v, recv_v, lax.rem(inner + d, n_inner))
                    return 0
                lax.fori_loop(0, n_inner, one, 0)

            @pl.when(e != 1)
            def _():
                base = jnp.where(e == 0, 0, n_inner + group_of(e) * n_inner)
                for h in range(n_inner):
                    y = y_buf[:, h * hd:(h + 1) * hd]
                    r = (y * cos_ref[...] + pltpu.roll(y, hd // 2, 1) * sin_ref[...]).astype(BF16)
                    for half in range(2):
                        qk_send[half, base + h] = r[half * chunk:(half + 1) * chunk]

            @pl.when(e == 0)
            def _():
                def one(d, _):
                    exchange(functools.partial(k_copy, sem_peer=None), send_k, recv_k, lax.rem(inner + d, n_inner))
                    return 0
                lax.fori_loop(0, n_inner, one, 0)

            @pl.when(e >= 2)
            def _():
                first = group_of(e) * (n_inner // groups)

                def one(d, _):
                    exchange(q_copy, send_q, recv_q, first + d)
                    return 0
                lax.fori_loop(0, n_inner // groups, one, 0)
            return 0
        lax.fori_loop(0, groups + 2, step, 0)

    pl.run_scoped(project, pltpu.VMEM((2, model, n_inner, hd), BF16), pltpu.VMEM((rows, n_inner * hd), F32))

    kv_landed()
    for part in range(4):
        y_send(outer, part, 0, 0, up).start()
        y_send(outer, part, 1, 1, down).start()

    def attend(w_buf, s0, s1, qt, m_buf, l_buf, acc):
        wide = w_buf.shape[2]

        def out_weights(c, slot):
            return pltpu.make_async_copy(wo_ref.at[:, pl.ds(pl.multiple_of(c * wide, wide), wide)], w_buf.at[slot], w_sem.at[slot])

        for c in range(2):
            out_weights(c, c).start()

        def q_landed(src, _):
            for half in range(2):
                landed(q_all.at[half, :, half_rows(half, src), :], recv_q.at[half, src])
            return 0
        lax.fori_loop(0, n_inner, q_landed, 0)

        def qk(s_buf, unit):
            side, t, kb, _ = unit
            s_buf[...] = jnp.dot(k_all[kb], qt[side * n_tiles + t], preferred_element_type=F32)

        def soft(s_buf, unit):
            side, t, kb, masked = unit
            idx = side * n_tiles + t
            s = s_buf[...]
            if masked:
                key = lax.broadcasted_iota(jnp.int32, s.shape, 0)
                pos = lax.rem(lax.broadcasted_iota(jnp.int32, s.shape, 1), tile) + t * tile
                s = jnp.where(key <= pos, s, NEG_BIG)
            m_old = m_buf[idx]
            m_new = jnp.maximum(m_old, s.max(axis=0, keepdims=True))
            p = jnp.exp2((s - m_new) * scale)
            rescale = jnp.exp2((m_old - m_new) * scale)
            m_buf[idx] = m_new
            l_buf[idx] = l_buf[idx] * rescale + p.sum(axis=0, keepdims=True)
            acc[idx] = acc[idx] * rescale + jnp.dot(v_all[kb], p.astype(BF16), preferred_element_type=F32)

        def run(units):
            bufs = (s0, s1)
            qk(bufs[0], units[0])
            for n, unit in enumerate(units):
                if n + 1 < len(units):
                    qk(bufs[(n + 1) % 2], units[n + 1])
                soft(bufs[n % 2], unit)

        def own(t, _):
            for side in range(2):
                idx = side * n_tiles + t
                for h in range(per_kv):
                    piece = q_all[side, h, pl.ds(pl.multiple_of(t * tile, tile), tile), :]
                    qt[idx, :, h * tile:(h + 1) * tile] = piece.T
                m_buf[idx] = jnp.full((1, cols), NEG_BIG, F32)
                l_buf[idx] = jnp.zeros((1, cols), F32)
                acc[idx] = jnp.zeros((hd, cols), F32)
            run([(0, t, outer, True), (1, t, mirror - outer, True), (1, t, outer, False)])
            return 0
        lax.fori_loop(0, n_tiles, own, 0)

        for part in range(4):
            landed(y_parts(down)[part], recv_y.at[0, part])
            landed(y_parts(up)[part], recv_y.at[1, part])
        for part in range(2):
            y_send(down, part, 2, 2, up).start()
            y_send(up, part + 2, 2, 2, down).start()

        def source(src, t):
            earlier = src < outer
            return [(jnp.where(earlier, 0, 1), t, src, False), (1, t, jnp.where(earlier, src, mirror - src), False)]

        def neighbour(t, _):
            run(source(down, t))
            return 0
        lax.fori_loop(0, n_tiles, neighbour, 0)

        for part in range(4):
            landed(y_parts(far)[part], recv_y.at[2, part])

        def o_copy(half, t, j):
            c = 2 * t + j
            peer = c if half == 0 else n_inner - 1 - c
            src = o_stage.at[half, t, pl.ds(j * chunk, chunk), :]
            dst = o_all.at[pl.ds(half * chunk, chunk), pl.ds(pl.multiple_of(inner * per_kv * hd, per_kv * hd), per_kv * hd)]
            return peer, src, dst

        def last(t, _):
            run(source(up, t) + source(far, t))
            for half in range(2):
                idx = half * n_tiles + t
                o_t = acc[idx] / l_buf[idx]
                for h in range(per_kv):
                    o_stage[half, t, :, h * hd:(h + 1) * hd] = o_t[:, h * tile:(h + 1) * tile].T.astype(BF16)
                for j in range(2):
                    peer, src, dst = o_copy(half, t, j)

                    @pl.when(peer != inner)
                    def _():
                        pltpu.make_async_remote_copy(src_ref=src, dst_ref=dst, send_sem=send_o.at[half, peer],
                                                     recv_sem=recv_o.at[half, inner], device_id=across(peer),
                                                     device_id_type=MESH).start()

                    @pl.when(peer == inner)
                    def _():
                        pltpu.make_async_copy(src, dst, recv_o.at[half, inner]).start()
            return 0
        lax.fori_loop(0, n_tiles, last, 0)

        def o_landed(src, _):
            for half in range(2):
                landed(o_all.at[pl.ds(half * chunk, chunk), pl.ds(pl.multiple_of(src * per_kv * hd, per_kv * hd), per_kv * hd)],
                       recv_o.at[half, src])
            return 0
        lax.fori_loop(0, n_inner, o_landed, 0)
        n_wide = model // wide

        def out_step(c, _):
            slot = lax.rem(c, 2)
            out_weights(c, slot).wait()
            res = jnp.dot(o_all[...], w_buf[slot], preferred_element_type=F32)
            out_ref[:, pl.ds(pl.multiple_of(c * wide, wide), wide)] = res.astype(BF16)

            @pl.when(c + 2 < n_wide)
            def _():
                out_weights(c + 2, slot).start()
            return 0
        lax.fori_loop(0, n_wide, out_step, 0)

        def sent(d, _):
            peer = lax.rem(inner + d, n_inner)
            heads = pl.ds(n_inner + peer * per_kv, per_kv)
            for half in range(2):
                landed(qk_send.at[half, peer], send_k.at[half, peer])
                landed(v_send.at[half, peer], send_v.at[half, peer])
                landed(qk_send.at[half, heads], send_q.at[half, peer])
                landed(o_stage.at[half, 0, pl.ds(0, chunk), :], send_o.at[half, peer])
            return 0
        lax.fori_loop(1, n_inner, sent, 0)
        for slot in range(3):
            for part in range(4):
                landed(y_parts(outer)[part], send_y.at[slot, part])

    pl.run_scoped(attend, pltpu.VMEM((2, wo_ref.shape[0], 1024), BF16), pltpu.VMEM((block, cols), F32),
                  pltpu.VMEM((block, cols), F32), pltpu.VMEM((2 * n_tiles, hd, cols), BF16),
                  pltpu.VMEM((2 * n_tiles, 1, cols), F32), pltpu.VMEM((2 * n_tiles, 1, cols), F32),
                  pltpu.VMEM((2 * n_tiles, hd, cols), F32))


def solution(mesh):
    n_outer = mesh.shape['cpo']
    n_inner = mesh.shape['cpi']
    n_dev = n_outer * n_inner

    def device_step(hidden, w_query, w_key, w_value, w_out):
        rows, model = hidden.shape
        chunk = rows // 2
        q_heads, hd = w_query.shape[1:]
        per_kv = q_heads // n_inner
        block = n_inner * chunk
        n_tiles = block // (2 * chunk)
        rank = lax.axis_index('cpo') * n_inner + lax.axis_index('cpi')
        offsets = jnp.arange(chunk, dtype=jnp.int32)
        positions = jnp.concatenate([rank * chunk + offsets, (2 * n_dev - 1 - rank) * chunk + offsets])
        cos, sin = rope_tables(positions, hd)
        cos2 = jnp.concatenate([cos, cos], axis=1)
        sin2 = jnp.concatenate([-sin, sin], axis=1)
        dma = pltpu.SemaphoreType.DMA
        pair = dma((2, n_inner))
        vmem = pl.BlockSpec(memory_space=pltpu.VMEM)
        hbm = pl.BlockSpec(memory_space=pl.ANY)
        return pl.pallas_call(
            functools.partial(layer_kernel, n_outer, n_inner),
            out_shape=jax.ShapeDtypeStruct((rows, model), BF16),
            in_specs=[vmem] * 3 + [hbm] * 4,
            out_specs=vmem,
            scratch_shapes=[
                pltpu.VMEM((2, n_inner + q_heads, chunk, hd), BF16),
                pltpu.VMEM((2, n_inner, hd, chunk), BF16),
                pltpu.VMEM((2 * n_outer, block, hd), BF16),
                pltpu.VMEM((2 * n_outer, hd, block), BF16),
                pltpu.VMEM((2, per_kv, block, hd), BF16),
                pltpu.VMEM((2, n_tiles, 2 * chunk, per_kv * hd), BF16),
                pltpu.VMEM((rows, q_heads * hd), BF16),
                dma((2,)), pair, pair, pair, pair, pair, pair, pair, pair, dma((3, 4)), dma((3, 4)),
            ],
            compiler_params=pltpu.CompilerParams(collective_id=0, has_side_effects=True, vmem_limit_bytes=66 * 1000 * 1000),
        )(hidden, cos2, sin2, w_query, w_key, w_value, w_out.reshape(q_heads * hd, model))

    row_spec = P(('dp', 'cpo', 'cpi'), None)
    weight_spec = P(None, None, None)
    return jax.shard_map(device_step, mesh=mesh, in_specs=(row_spec, weight_spec, weight_spec, weight_spec, weight_spec), out_specs=row_spec, check_vma=False)
```

time: 505 us -> 127 us (0.25); the launches traced: 496 us -> 126 us
  matrix products: 178 us -> 0 us
  Pallas kernels: 0 us -> 121 us
  waiting for transfers between devices: 97 us -> 0 us
  local copies, waits for them, and re-layouts: 87.5 us -> 3.13 us
  other arithmetic: 79.9 us -> 2.09 us
  blocking collectives: 32.1 us -> 0 us
  starting transfers between devices: 20.4 us -> 0 us
    dot_general x14 -> x0, matrix products: 178 us -> none  [the longest x5 72.7 us: softmax_update(): jnp.einsum('qkgs,skd->qkgd', probs_blk.astype(jnp.bfloat16), values_blk,...]
    pallas_call x0 -> x1, Pallas kernels: none -> 121 us  [device_step(): pl.pallas_call(functools.partial(layer_kernel, n_outer, n_inner), out_sha...]
    ppermute x6 -> x0, waiting for transfers between devices: 70.7 us -> none  [outer_step(): kv_block = lax.ppermute(kv_block, 'cpo', shift_perm)]
    reduce_sum x5 -> x0, other arithmetic: 61 us -> none  [softmax_update(): new_sum = run_sum * rescale + probs_blk.sum(axis=-1)]
    unnamed x18 -> x1, local copies, waits for them, and re-layouts: 60.6 us -> 3.13 us
    all_to_all x1 -> x0, blocking collectives: 32.1 us -> none  [device_step(): lax.all_to_all(out_heads, 'cpi', 1, 3, tiled=True)]
    all_to_all x3 -> x0, waiting for transfers between devices: 26.3 us -> none  [to_heads(): tensor_in = lax.all_to_all(tensor_in, 'cpi', 3, 1, tiled=True)]
    all_to_all x3 -> x0, starting transfers between devices: 16.6 us -> none  [to_heads(): tensor_in = lax.all_to_all(tensor_in, 'cpi', 3, 1, tiled=True)]
  transfers between devices with their start and end apart: 9 -> 0, of which waited for: 8 -> 0; matrix products, arithmetic and copies ran while one was open for 15% -> 0% of each run, Pallas kernels for 0% -> 0%
where the time goes in v1:
time: 127 us; the launch traced here: 126 us
  Pallas kernels  121 us (95%)
  local copies, waits for them, and re-layouts  3.13 us (2%)
  other arithmetic  2.09 us (2%)
    pallas_call x1, Pallas kernels, device_step(): pl.pallas_call(functools.partial(layer_kernel, n_outer, n_inner), out_sha...  121 us
    unnamed x1, local copies, waits for them, and re-layouts  3.13 us

profile of v1, /device:TPU:97, one launch (start us, length us, event | category | flops | bytes accessed | tf_op | source)
XLA Modules:
  0.0 126.4 jit_solution(9856051752013722125)
XLA Ops:
  0.0 0.5 fusion
  0.6 0.8 pad_maximum_fusion.1.sin_ref
  1.3 0.8 pad_maximum_fusion.cos_ref
  2.1 121.1 %shard_map.55 = bf16[256,4096]{1,0:T(8,128)(2,1)} custom-call(bf16[256,4096]{1,0:T(8,128)(2,1)} %x_ref.1, f32[256,128]{1,0:T(8,128)} %pad_maximum_fusion.cos_ref, f32[256,128]{1,0:T(8,128)} %pad_maximum_fusion.1.sin_ref, bf16[4096,32,128]{2,1,0:T(8,128)(2,1)} %wq_ref.1, bf16[4096,8,128]{2,1,0:T(8,128)(2,1)} %wk_ref.1, bf16[4096,8,128]{2,1,0:T(8,128)(2,1)} %wv_ref.1, ...), custom_call_target="tpu_custom_call" | custom-call | tf_op jit(solution)/shard_map/pallas_call | solution.py:353
  123.2 3.1 %copy.7 = bf16[256,4096]{1,0:T(8,128)(2,1)} copy(bf16[256,4096]{1,0:T(8,128)(2,1)} %shard_map.55) | data formatting | bytes 4194304
  (3 shorter events, 0.0 us)

commit v2 on v1

--- a/solution.py
+++ b/solution.py
@@ -17,9 +17,10 @@
 
 def rope_tables(positions, head_dim):
     half_dim = head_dim // 2
-    inv_freq = ROPE_BASE ** (-(2.0 / head_dim) * jnp.arange(half_dim, dtype=F32))
-    angles = positions.astype(F32)[..., None] * inv_freq
-    return jnp.cos(angles), jnp.sin(angles)
+    lane = jnp.arange(head_dim, dtype=jnp.int32)
+    inv_freq = ROPE_BASE ** (-(2.0 / head_dim) * (lane % half_dim).astype(F32))
+    angles = positions.astype(F32)[:, None] * inv_freq
+    return jnp.cos(angles), jnp.where(lane < half_dim, -jnp.sin(angles), jnp.sin(angles))
 
 
 def layer_kernel(n_outer, n_inner, x_ref, cos_ref, sin_ref, wq_ref, wk_ref, wv_ref, wo_ref, out_ref,
@@ -43,6 +44,11 @@
     far = lax.rem(outer + 2, n_outer)
     mirror = n_blocks - 1
 
+    here = inner // (n_inner // groups)
+
+    def beyond(hops):
+        return lax.rem(here + hops, groups)
+
     def across(peer):
         return {"cpi": peer}
 
@@ -65,7 +71,7 @@
         start = who * chunk if half == 0 else (n_inner - 1 - who) * chunk
         return pl.ds(pl.multiple_of(start, chunk), chunk)
 
-    def k_copy(half, peer, owner, sem_peer):
+    def k_copy(half, peer, owner):
         return dict(src_ref=qk_send.at[half, peer], dst_ref=k_all.at[half_block(half, outer), half_rows(half, owner), :])
 
     def v_copy(half, peer, owner):
@@ -89,13 +95,15 @@
                 refs = make(half, peer, inner)
                 pltpu.make_async_copy(refs["src_ref"], refs["dst_ref"], recv.at[half, inner]).start()
 
-    def kv_landed():
-        def one(src, _):
-            for half in range(2):
-                landed(k_all.at[half_block(half, outer), half_rows(half, src), :], recv_k.at[half, src])
-                landed(v_all.at[half_block(half, outer), :, half_rows(half, src)], recv_v.at[half, src])
-            return 0
-        lax.fori_loop(0, n_inner, one, 0)
+    def k_landed(src, _):
+        for half in range(2):
+            landed(k_all.at[half_block(half, outer), half_rows(half, src), :], recv_k.at[half, src])
+        return 0
+
+    def v_landed(src, _):
+        for half in range(2):
+            landed(v_all.at[half_block(half, outer), :, half_rows(half, src)], recv_v.at[half, src])
+        return 0
 
     def y_parts(src):
         return (k_all.at[src], k_all.at[mirror - src], v_all.at[src], v_all.at[mirror - src])
@@ -123,7 +131,7 @@
                 do(pltpu.make_async_copy(wq_ref.at[:, heads, :], w_buf.at[slot], w_sem.at[slot]))
 
         def group_of(e):
-            return lax.rem(inner * groups // n_inner + e, groups)
+            return beyond(jnp.where(e == 2, 1, jnp.where(e == 3, 3, jnp.where(e == 4, 2, 0))))
 
         fetch(0, lambda c: c.start())
         fetch(1, lambda c: c.start())
@@ -162,7 +170,7 @@
             @pl.when(e == 0)
             def _():
                 def one(d, _):
-                    exchange(functools.partial(k_copy, sem_peer=None), send_k, recv_k, lax.rem(inner + d, n_inner))
+                    exchange(k_copy, send_k, recv_k, lax.rem(inner + d, n_inner))
                     return 0
                 lax.fori_loop(0, n_inner, one, 0)
 
@@ -174,15 +182,18 @@
                     exchange(q_copy, send_q, recv_q, first + d)
                     return 0
                 lax.fori_loop(0, n_inner // groups, one, 0)
+
+            for when, here_yet, parts in ((3, k_landed, (0, 1)), (4, v_landed, (2, 3))):
+                @pl.when(e == when)
+                def _():
+                    lax.fori_loop(0, n_inner, here_yet, 0)
+                    for part in parts:
+                        y_send(outer, part, 0, 0, up).start()
+                        y_send(outer, part, 1, 1, down).start()
             return 0
         lax.fori_loop(0, groups + 2, step, 0)
 
     pl.run_scoped(project, pltpu.VMEM((2, model, n_inner, hd), BF16), pltpu.VMEM((rows, n_inner * hd), F32))
-
-    kv_landed()
-    for part in range(4):
-        y_send(outer, part, 0, 0, up).start()
-        y_send(outer, part, 1, 1, down).start()
 
     def attend(w_buf, s0, s1, qt, m_buf, l_buf, acc):
         wide = w_buf.shape[2]
@@ -193,23 +204,24 @@
         for c in range(2):
             out_weights(c, c).start()
 
-        def q_landed(src, _):
-            for half in range(2):
-                landed(q_all.at[half, :, half_rows(half, src), :], recv_q.at[half, src])
-            return 0
-        lax.fori_loop(0, n_inner, q_landed, 0)
-
         def qk(s_buf, unit):
-            side, t, kb, _ = unit
-            s_buf[...] = jnp.dot(k_all[kb], qt[side * n_tiles + t], preferred_element_type=F32)
+            side, t, kb, quarter = unit
+            if quarter is None:
+                s_buf[...] = jnp.dot(k_all[kb], qt[side * n_tiles + t], preferred_element_type=F32)
+            else:
+                keys = pl.ds(pl.multiple_of(quarter * tile, tile), tile)
+                s_buf[:tile] = jnp.dot(k_all[kb, keys, :], qt[side * n_tiles + t], preferred_element_type=F32)
 
         def soft(s_buf, unit):
-            side, t, kb, masked = unit
+            side, t, kb, quarter = unit
             idx = side * n_tiles + t
-            s = s_buf[...]
-            if masked:
-                key = lax.broadcasted_iota(jnp.int32, s.shape, 0)
-                pos = lax.rem(lax.broadcasted_iota(jnp.int32, s.shape, 1), tile) + t * tile
+            if quarter is None:
+                s, v = s_buf[...], v_all[kb]
+            else:
+                keys = pl.ds(pl.multiple_of(quarter * tile, tile), tile)
+                s, v = s_buf[:tile], v_all[kb, :, keys]
+                key = lax.broadcasted_iota(jnp.int32, s.shape, 0) + (quarter - t) * tile
+                pos = lax.rem(lax.broadcasted_iota(jnp.int32, s.shape, 1), tile)
                 s = jnp.where(key <= pos, s, NEG_BIG)
             m_old = m_buf[idx]
             m_new = jnp.maximum(m_old, s.max(axis=0, keepdims=True))
@@ -217,18 +229,42 @@
             rescale = jnp.exp2((m_old - m_new) * scale)
             m_buf[idx] = m_new
             l_buf[idx] = l_buf[idx] * rescale + p.sum(axis=0, keepdims=True)
-            acc[idx] = acc[idx] * rescale + jnp.dot(v_all[kb], p.astype(BF16), preferred_element_type=F32)
-
-        def run(units):
+            acc[idx] = acc[idx] * rescale + jnp.dot(v, p.astype(BF16), preferred_element_type=F32)
+
+        def run(units, before=None):
             bufs = (s0, s1)
             qk(bufs[0], units[0])
             for n, unit in enumerate(units):
                 if n + 1 < len(units):
+                    if before and n + 1 in before:
+                        before[n + 1]()
                     qk(bufs[(n + 1) % 2], units[n + 1])
                 soft(bufs[n % 2], unit)
 
-        def own(t, _):
+        def own(step, _):
+            chip = beyond(jnp.where(step == 2, 3, jnp.where(step == 3, 2, step)))
+            t_side = (chip, n_tiles - 1 - chip)
+
+            def q_landed(src, _):
+                for half in range(2):
+                    landed(q_all.at[half, :, half_rows(half, src), :], recv_q.at[half, src])
+                return 0
+            lax.fori_loop(chip * (n_inner // groups), (chip + 1) * (n_inner // groups), q_landed, 0)
+
+            @pl.when(step == 2)
+            def _():
+                for part in (0, 1):
+                    landed(y_parts(down)[part], recv_y.at[0, part])
+                    y_send(down, part, 2, 2, up).start()
+
+            @pl.when(step == 3)
+            def _():
+                for part in (2, 3):
+                    landed(y_parts(up)[part], recv_y.at[1, part])
+                    y_send(up, part, 2, 2, down).start()
+
             for side in range(2):
+                t = t_side[side]
                 idx = side * n_tiles + t
                 for h in range(per_kv):
                     piece = q_all[side, h, pl.ds(pl.multiple_of(t * tile, tile), tile), :]
@@ -236,28 +272,24 @@
                 m_buf[idx] = jnp.full((1, cols), NEG_BIG, F32)
                 l_buf[idx] = jnp.zeros((1, cols), F32)
                 acc[idx] = jnp.zeros((hd, cols), F32)
-            run([(0, t, outer, True), (1, t, mirror - outer, True), (1, t, outer, False)])
+            units = []
+            for n in range(n_tiles + 1):
+                front = n <= chip
+                units.append((jnp.where(front, 0, 1), jnp.where(front, t_side[0], t_side[1]),
+                              jnp.where(front, outer, mirror - outer), jnp.where(front, n, n - chip - 1)))
+            run(units + [(1, t_side[1], outer, None)])
             return 0
         lax.fori_loop(0, n_tiles, own, 0)
 
-        for part in range(4):
+        for part in (0, 1):
+            landed(y_parts(up)[part], recv_y.at[1, part])
+        for part in (2, 3):
             landed(y_parts(down)[part], recv_y.at[0, part])
-            landed(y_parts(up)[part], recv_y.at[1, part])
-        for part in range(2):
-            y_send(down, part, 2, 2, up).start()
-            y_send(up, part + 2, 2, 2, down).start()
-
-        def source(src, t):
+
+        def source(src, t_side):
             earlier = src < outer
-            return [(jnp.where(earlier, 0, 1), t, src, False), (1, t, jnp.where(earlier, src, mirror - src), False)]
-
-        def neighbour(t, _):
-            run(source(down, t))
-            return 0
-        lax.fori_loop(0, n_tiles, neighbour, 0)
-
-        for part in range(4):
-            landed(y_parts(far)[part], recv_y.at[2, part])
+            return [(jnp.where(earlier, 0, 1), jnp.where(earlier, t_side[0], t_side[1]), src, None),
+                    (1, t_side[1], jnp.where(earlier, src, mirror - src), None)]
 
         def o_copy(half, t, j):
             c = 2 * t + j
@@ -266,9 +298,19 @@
             dst = o_all.at[pl.ds(half * chunk, chunk), pl.ds(pl.multiple_of(inner * per_kv * hd, per_kv * hd), per_kv * hd)]
             return peer, src, dst
 
-        def last(t, _):
-            run(source(up, t) + source(far, t))
+        def last(step, _):
+            chip = beyond(jnp.where(step == 0, 2, jnp.where(step == 1, 1, jnp.where(step == 2, 3, 0))))
+            t_side = (chip, n_tiles - 1 - chip)
+
+            def far_landed():
+                @pl.when(step == 0)
+                def _():
+                    for part in range(4):
+                        landed(y_parts(far)[part], recv_y.at[2, part])
+
+            run(source(down, t_side) + source(up, t_side) + source(far, t_side), before={4: far_landed})
             for half in range(2):
+                t = t_side[half]
                 idx = half * n_tiles + t
                 o_t = acc[idx] / l_buf[idx]
                 for h in range(per_kv):
@@ -344,8 +386,6 @@
         offsets = jnp.arange(chunk, dtype=jnp.int32)
         positions = jnp.concatenate([rank * chunk + offsets, (2 * n_dev - 1 - rank) * chunk + offsets])
         cos, sin = rope_tables(positions, hd)
-        cos2 = jnp.concatenate([cos, cos], axis=1)
-        sin2 = jnp.concatenate([-sin, sin], axis=1)
         dma = pltpu.SemaphoreType.DMA
         pair = dma((2, n_inner))
         vmem = pl.BlockSpec(memory_space=pltpu.VMEM)
@@ -365,8 +405,8 @@
                 pltpu.VMEM((rows, q_heads * hd), BF16),
                 dma((2,)), pair, pair, pair, pair, pair, pair, pair, pair, dma((3, 4)), dma((3, 4)),
             ],
-            compiler_params=pltpu.CompilerParams(collective_id=0, has_side_effects=True, vmem_limit_bytes=66 * 1000 * 1000),
-        )(hidden, cos2, sin2, w_query, w_key, w_value, w_out.reshape(q_heads * hd, model))
+            compiler_params=pltpu.CompilerParams(collective_id=0, has_side_effects=True, vmem_limit_bytes=56 * 1024 * 1024),
+        )(hidden, cos, sin, w_query, w_key, w_value, w_out.reshape(q_heads * hd, model))
 
     row_spec = P(('dp', 'cpo', 'cpi'), None)
     weight_spec = P(None, None, None)

time: 127 us -> 109 us (0.86)
  Pallas kernels: 121 us -> 104 us
    pallas_call x1, Pallas kernels: 121 us -> 104 us  [device_step(): pl.pallas_call(functools.partial(layer_kernel, n_outer, n_inner), out_sha...]
    concatenate x2 -> x0, other arithmetic: 1.53 us -> none  [the longest x1 0.77 us: device_step(): sin2 = jnp.concatenate([-sin, sin], axis=1)]
where the time goes in v2:
time: 109 us; the launch traced here: 108 us
  Pallas kernels  104 us (95%)
  local copies, waits for them, and re-layouts  3.13 us (3%)
  other arithmetic  1.28 us (1%)
    pallas_call x1, Pallas kernels, device_step(): pl.pallas_call(functools.partial(layer_kernel, n_outer, n_inner), out_sha...  104 us
    unnamed x1, local copies, waits for them, and re-layouts  3.13 us

profile of v2, /device:TPU:97, one launch (start us, length us, event | category | flops | bytes accessed | tf_op | source)
XLA Modules:
  0.0 108.4 jit_solution(10050410844433790210)
XLA Ops:
  0.0 1.2 %negate_select_fusion = (f32[256,128]{1,0:T(8,128)}, f32[256,128]{1,0:T(8,128)}) fusion(f32[128]{0:T(128)S(1)} %fusion.2, f32[256]{0:T(256)S(1)} %add_convert_fusion, pred[128]{0:T(512)(128)(4,1)S(1)} %iota_compare_fusion), kind=kLoop, calls=%fused_computation | loop fusion | flops 98304 | bytes 263808 | tf_op jit(solution)/shard_map/jit(_where)/select_n | solution.py:23
  1.3 104.0 %shard_map.55 = bf16[256,4096]{1,0:T(8,128)(2,1)} custom-call(bf16[256,4096]{1,0:T(8,128)(2,1)} %x_ref.1, f32[256,128]{1,0:T(8,128)} %get-tuple-element.6.cos_ref, f32[256,128]{1,0:T(8,128)} %get-tuple-element.5.sin_ref, bf16[4096,32,128]{2,1,0:T(8,128)(2,1)} %wq_ref.1, bf16[4096,8,128]{2,1,0:T(8,128)(2,1)} %wk_ref.1, bf16[4096,8,128]{2,1,0:T(8,128)(2,1)} %wv_ref.1, ...), custom_call_target="tpu_custom_call" | custom-call | tf_op jit(solution)/shard_map/pallas_call | solution.py:393
  105.3 3.1 %copy.7 = bf16[256,4096]{1,0:T(8,128)(2,1)} copy(bf16[256,4096]{1,0:T(8,128)(2,1)} %shard_map.55) | data formatting | bytes 4194304
  (4 shorter events, 0.0 us)

commit v3 on v2

--- a/solution.py
+++ b/solution.py
@@ -23,12 +23,12 @@
     return jnp.cos(angles), jnp.where(lane < half_dim, -jnp.sin(angles), jnp.sin(angles))
 
 
-def layer_kernel(n_outer, n_inner, x_ref, cos_ref, sin_ref, wq_ref, wk_ref, wv_ref, wo_ref, out_ref,
-                 qk_send, v_send, k_all, v_all, q_all, o_stage, o_all,
+def layer_kernel(n_outer, n_inner, x_hbm, cos_ref, sin_ref, wq_ref, wk_ref, wv_ref, wo_ref, out_ref,
+                 x_ref, qk_send, v_send, k_all, v_all, q_all, o_stage, o_all,
                  w_sem, send_k, recv_k, send_v, recv_v, send_q, recv_q, send_o, recv_o, send_y, recv_y):
     outer = lax.axis_index("cpo")
     inner = lax.axis_index("cpi")
-    rows, model = x_ref.shape
+    rows, model = x_hbm.shape
     chunk = rows // 2
     hd = cos_ref.shape[1]
     block = n_inner * chunk
@@ -38,6 +38,7 @@
     tile = 2 * chunk
     n_tiles = block // tile
     cols = per_kv * tile
+    piece = 2 * tile
     scale = LOG2E * hd ** -0.5
     up = lax.rem(outer + 1, n_outer)
     down = lax.rem(outer + n_outer - 1, n_outer)
@@ -113,114 +114,110 @@
         return pltpu.make_async_remote_copy(src_ref=ref, dst_ref=ref, send_sem=send_y.at[slot, part],
                                             recv_sem=recv_y.at[lane, part], device_id=along(peer), device_id_type=MESH)
 
-    def project(w_buf, y_buf):
-        def fetch(e, do):
-            slot = lax.rem(e, 2)
-
-            @pl.when(e == 0)
-            def _():
-                do(pltpu.make_async_copy(wk_ref, w_buf.at[slot], w_sem.at[slot]))
-
-            @pl.when(e == 1)
-            def _():
-                do(pltpu.make_async_copy(wv_ref, w_buf.at[slot], w_sem.at[slot]))
-
-            @pl.when(e >= 2)
-            def _():
-                heads = pl.ds(pl.multiple_of(group_of(e) * n_inner, n_inner), n_inner)
-                do(pltpu.make_async_copy(wq_ref.at[:, heads, :], w_buf.at[slot], w_sem.at[slot]))
-
-        def group_of(e):
-            return beyond(jnp.where(e == 2, 1, jnp.where(e == 3, 3, jnp.where(e == 4, 2, 0))))
-
-        fetch(0, lambda c: c.start())
-        fetch(1, lambda c: c.start())
+    def project(w_buf):
+        def group_of(n):
+            return beyond(jnp.where(n == 0, 1, jnp.where(n == 1, groups - 1, jnp.where(n == 2, 2, 0))))
+
+        def fetch_q(n, slot):
+            heads = pl.ds(pl.multiple_of(group_of(n) * n_inner, n_inner), n_inner)
+            return pltpu.make_async_copy(wq_ref.at[:, heads, :], w_buf.at[slot], w_sem.at[slot])
+
+        fetch_k = pltpu.make_async_copy(wk_ref, w_buf.at[0], w_sem.at[0])
+        fetch_v = pltpu.make_async_copy(wv_ref, w_buf.at[1], w_sem.at[1])
+        fetch_x = pltpu.make_async_copy(x_hbm, x_ref, w_sem.at[2])
+        fetch_x.start()
+        fetch_k.start()
         pl.semaphore_wait(barrier, n_inner + 1)
 
-        def step(e, _):
-            slot = lax.rem(e, 2)
-            fetch(e, lambda c: c.wait())
-            y_buf[...] = jnp.dot(x_ref[...], w_buf[slot].reshape(model, n_inner * hd), preferred_element_type=F32)
-
-            @pl.when(e + 2 < groups + 2)
-            def _():
-                fetch(e + 2, lambda c: c.start())
-
-            @pl.when(e == 1)
-            def _():
-                for h in range(n_inner):
-                    vt = y_buf[:, h * hd:(h + 1) * hd].T.astype(BF16)
-                    for half in range(2):
-                        v_send[half, h] = vt[:, half * chunk:(half + 1) * chunk]
-
-                def one(d, _):
-                    exchange(v_copy, send_v, recv_v, lax.rem(inner + d, n_inner))
-                    return 0
-                lax.fori_loop(0, n_inner, one, 0)
-
-            @pl.when(e != 1)
-            def _():
-                base = jnp.where(e == 0, 0, n_inner + group_of(e) * n_inner)
-                for h in range(n_inner):
-                    y = y_buf[:, h * hd:(h + 1) * hd]
-                    r = (y * cos_ref[...] + pltpu.roll(y, hd // 2, 1) * sin_ref[...]).astype(BF16)
-                    for half in range(2):
-                        qk_send[half, base + h] = r[half * chunk:(half + 1) * chunk]
-
-            @pl.when(e == 0)
-            def _():
-                def one(d, _):
-                    exchange(k_copy, send_k, recv_k, lax.rem(inner + d, n_inner))
-                    return 0
-                lax.fori_loop(0, n_inner, one, 0)
-
-            @pl.when(e >= 2)
-            def _():
-                first = group_of(e) * (n_inner // groups)
-
-                def one(d, _):
-                    exchange(q_copy, send_q, recv_q, first + d)
-                    return 0
-                lax.fori_loop(0, n_inner // groups, one, 0)
-
-            for when, here_yet, parts in ((3, k_landed, (0, 1)), (4, v_landed, (2, 3))):
-                @pl.when(e == when)
+        def product(slot):
+            return jnp.dot(x_ref[...], w_buf[slot].reshape(model, n_inner * hd), preferred_element_type=F32)
+
+        def rotate_store(y_all, base):
+            for h in range(n_inner):
+                y = y_all[:, h * hd:(h + 1) * hd]
+                r = (y * cos_ref[...] + pltpu.roll(y, hd // 2, 1) * sin_ref[...]).astype(BF16)
+                for half in range(2):
+                    qk_send[half, base + h] = r[half * chunk:(half + 1) * chunk]
+
+        def to_all(make, send, recv):
+            def one(d, _):
+                exchange(make, send, recv, lax.rem(inner + d, n_inner))
+                return 0
+            lax.fori_loop(0, n_inner, one, 0)
+
+        fetch_x.wait()
+        fetch_k.wait()
+        fetch_v.start()
+        rotate_store(product(0), 0)
+        to_all(k_copy, send_k, recv_k)
+
+        fetch_v.wait()
+        fetch_q(0, 0).start()
+        y_all = product(1)
+        for h in range(n_inner):
+            vt = y_all[:, h * hd:(h + 1) * hd].T.astype(BF16)
+            for half in range(2):
+                v_send[half, h] = vt[:, half * chunk:(half + 1) * chunk]
+        fetch_q(1, 1).start()
+        to_all(v_copy, send_v, recv_v)
+
+        def step(n, _):
+            slot = lax.rem(n, 2)
+            fetch_q(n, slot).wait()
+            first = group_of(n)
+            rotate_store(product(slot), n_inner + first * n_inner)
+
+            @pl.when(n + 2 < groups)
+            def _():
+                fetch_q(n + 2, slot).start()
+
+            def one(d, _):
+                exchange(q_copy, send_q, recv_q, first * (n_inner // groups) + d)
+                return 0
+            lax.fori_loop(0, n_inner // groups, one, 0)
+
+            for when, here_yet, parts in ((1, k_landed, (0, 1)), (groups - 1, v_landed, (2, 3))):
+                @pl.when(n == when)
                 def _():
                     lax.fori_loop(0, n_inner, here_yet, 0)
                     for part in parts:
                         y_send(outer, part, 0, 0, up).start()
                         y_send(outer, part, 1, 1, down).start()
             return 0
-        lax.fori_loop(0, groups + 2, step, 0)
-
-    pl.run_scoped(project, pltpu.VMEM((2, model, n_inner, hd), BF16), pltpu.VMEM((rows, n_inner * hd), F32))
-
-    def attend(w_buf, s0, s1, qt, m_buf, l_buf, acc):
-        wide = w_buf.shape[2]
+        lax.fori_loop(0, groups, step, 0)
+
+    pl.run_scoped(project, pltpu.VMEM((2, model, n_inner, hd), BF16))
+
+    def attend(w_buf, total, s0, s1, qt, m_buf, l_buf, acc):
+        deep = w_buf.shape[1]
+
+        def out_chip(c):
+            return beyond(jnp.where(c == 1, 2, jnp.where(c == 2, 1, jnp.where(c == 3, groups - 1, 0))))
 
         def out_weights(c, slot):
-            return pltpu.make_async_copy(wo_ref.at[:, pl.ds(pl.multiple_of(c * wide, wide), wide)], w_buf.at[slot], w_sem.at[slot])
+            rows_of = pl.ds(pl.multiple_of(out_chip(c) * deep, deep), deep)
+            return pltpu.make_async_copy(wo_ref.at[rows_of, :], w_buf.at[slot], w_sem.at[slot])
 
         for c in range(2):
             out_weights(c, c).start()
 
         def qk(s_buf, unit):
-            side, t, kb, quarter = unit
-            if quarter is None:
+            side, t, kb, part_of = unit
+            if part_of is None:
                 s_buf[...] = jnp.dot(k_all[kb], qt[side * n_tiles + t], preferred_element_type=F32)
             else:
-                keys = pl.ds(pl.multiple_of(quarter * tile, tile), tile)
-                s_buf[:tile] = jnp.dot(k_all[kb, keys, :], qt[side * n_tiles + t], preferred_element_type=F32)
+                keys = pl.ds(pl.multiple_of(part_of * piece, piece), piece)
+                s_buf[:piece] = jnp.dot(k_all[kb, keys, :], qt[side * n_tiles + t], preferred_element_type=F32)
 
         def soft(s_buf, unit):
-            side, t, kb, quarter = unit
+            side, t, kb, part_of = unit
             idx = side * n_tiles + t
-            if quarter is None:
+            if part_of is None:
                 s, v = s_buf[...], v_all[kb]
             else:
-                keys = pl.ds(pl.multiple_of(quarter * tile, tile), tile)
-                s, v = s_buf[:tile], v_all[kb, :, keys]
-                key = lax.broadcasted_iota(jnp.int32, s.shape, 0) + (quarter - t) * tile
+                keys = pl.ds(pl.multiple_of(part_of * piece, piece), piece)
+                s, v = s_buf[:piece], v_all[kb, :, keys]
+                key = lax.broadcasted_iota(jnp.int32, s.shape, 0) + (part_of * piece - t * tile)
                 pos = lax.rem(lax.broadcasted_iota(jnp.int32, s.shape, 1), tile)
                 s = jnp.where(key <= pos, s, NEG_BIG)
             m_old = m_buf[idx]
@@ -231,19 +228,23 @@
             l_buf[idx] = l_buf[idx] * rescale + p.sum(axis=0, keepdims=True)
             acc[idx] = acc[idx] * rescale + jnp.dot(v, p.astype(BF16), preferred_element_type=F32)
 
-        def run(units, before=None):
+        def run(units):
             bufs = (s0, s1)
             qk(bufs[0], units[0])
             for n, unit in enumerate(units):
                 if n + 1 < len(units):
-                    if before and n + 1 in before:
-                        before[n + 1]()
                     qk(bufs[(n + 1) % 2], units[n + 1])
                 soft(bufs[n % 2], unit)
 
         def own(step, _):
             chip = beyond(jnp.where(step == 2, 3, jnp.where(step == 3, 2, step)))
             t_side = (chip, n_tiles - 1 - chip)
+
+            @pl.when(step == 2)
+            def _():
+                for part in (0, 1):
+                    landed(y_parts(down)[part], recv_y.at[0, part])
+                    y_send(down, part, 2, 2, up).start()
 
             def q_landed(src, _):
                 for half in range(2):
@@ -251,36 +252,28 @@
                 return 0
             lax.fori_loop(chip * (n_inner // groups), (chip + 1) * (n_inner // groups), q_landed, 0)
 
-            @pl.when(step == 2)
-            def _():
-                for part in (0, 1):
-                    landed(y_parts(down)[part], recv_y.at[0, part])
-                    y_send(down, part, 2, 2, up).start()
-
-            @pl.when(step == 3)
-            def _():
-                for part in (2, 3):
-                    landed(y_parts(up)[part], recv_y.at[1, part])
-                    y_send(up, part, 2, 2, down).start()
-
             for side in range(2):
                 t = t_side[side]
                 idx = side * n_tiles + t
                 for h in range(per_kv):
-                    piece = q_all[side, h, pl.ds(pl.multiple_of(t * tile, tile), tile), :]
-                    qt[idx, :, h * tile:(h + 1) * tile] = piece.T
+                    q_tile = q_all[side, h, pl.ds(pl.multiple_of(t * tile, tile), tile), :]
+                    qt[idx, :, h * tile:(h + 1) * tile] = q_tile.T
                 m_buf[idx] = jnp.full((1, cols), NEG_BIG, F32)
                 l_buf[idx] = jnp.zeros((1, cols), F32)
                 acc[idx] = jnp.zeros((hd, cols), F32)
             units = []
-            for n in range(n_tiles + 1):
-                front = n <= chip
+            for n in range(n_tiles // 2 + 1):
+                last_front = chip * tile // piece
+                front = n <= last_front
                 units.append((jnp.where(front, 0, 1), jnp.where(front, t_side[0], t_side[1]),
-                              jnp.where(front, outer, mirror - outer), jnp.where(front, n, n - chip - 1)))
+                              jnp.where(front, outer, mirror - outer), jnp.where(front, n, n - last_front - 1)))
             run(units + [(1, t_side[1], outer, None)])
             return 0
         lax.fori_loop(0, n_tiles, own, 0)
 
+        for part in (2, 3):
+            landed(y_parts(up)[part], recv_y.at[1, part])
+            y_send(up, part, 2, 2, down).start()
         for part in (0, 1):
             landed(y_parts(up)[part], recv_y.at[1, part])
         for part in (2, 3):
@@ -298,17 +291,28 @@
             dst = o_all.at[pl.ds(half * chunk, chunk), pl.ds(pl.multiple_of(inner * per_kv * hd, per_kv * hd), per_kv * hd)]
             return peer, src, dst
 
+        def by_distance(step):
+            return beyond(jnp.where(step == 0, 2, jnp.where(step == 1, 1, jnp.where(step == 2, groups - 1, 0))))
+
+        def neighbours(step, _):
+            chip = by_distance(step)
+            t_side = (chip, n_tiles - 1 - chip)
+            run(source(down, t_side) + source(up, t_side))
+            return 0
+        lax.fori_loop(0, 2, neighbours, 0)
+
+        for part in range(4):
+            landed(y_parts(far)[part], recv_y.at[2, part])
+
         def last(step, _):
-            chip = beyond(jnp.where(step == 0, 2, jnp.where(step == 1, 1, jnp.where(step == 2, 3, 0))))
+            chip = by_distance(step)
             t_side = (chip, n_tiles - 1 - chip)
 
-            def far_landed():
-                @pl.when(step == 0)
-                def _():
-                    for part in range(4):
-                        landed(y_parts(far)[part], recv_y.at[2, part])
-
-            run(source(down, t_side) + source(up, t_side) + source(far, t_side), before={4: far_landed})
+            @pl.when(step >= 2)
+            def _():
+                run(source(down, t_side) + source(up, t_side))
+
+            run(source(far, t_side))
             for half in range(2):
                 t = t_side[half]
                 idx = half * n_tiles + t
@@ -335,20 +339,30 @@
                 landed(o_all.at[pl.ds(half * chunk, chunk), pl.ds(pl.multiple_of(src * per_kv * hd, per_kv * hd), per_kv * hd)],
                        recv_o.at[half, src])
             return 0
-        lax.fori_loop(0, n_inner, o_landed, 0)
-        n_wide = model // wide
 
         def out_step(c, _):
             slot = lax.rem(c, 2)
+            chip = out_chip(c)
+            per_chip = n_inner // groups
+            lax.fori_loop(chip * per_chip, (chip + 1) * per_chip, o_landed, 0)
             out_weights(c, slot).wait()
-            res = jnp.dot(o_all[...], w_buf[slot], preferred_element_type=F32)
-            out_ref[:, pl.ds(pl.multiple_of(c * wide, wide), wide)] = res.astype(BF16)
-
-            @pl.when(c + 2 < n_wide)
+            here_cols = pl.ds(pl.multiple_of(chip * deep, deep), deep)
+            part = jnp.dot(o_all[:, here_cols], w_buf[slot], preferred_element_type=F32)
+
+            @pl.when(c == 0)
+            def _():
+                total[...] = part
+
+            @pl.when(c > 0)
+            def _():
+                total[...] += part
+
+            @pl.when(c + 2 < groups)
             def _():
                 out_weights(c + 2, slot).start()
             return 0
-        lax.fori_loop(0, n_wide, out_step, 0)
+        lax.fori_loop(0, groups, out_step, 0)
+        out_ref[...] = total[...].astype(BF16)
 
         def sent(d, _):
             peer = lax.rem(inner + d, n_inner)
@@ -364,7 +378,7 @@
             for part in range(4):
                 landed(y_parts(outer)[part], send_y.at[slot, part])
 
-    pl.run_scoped(attend, pltpu.VMEM((2, wo_ref.shape[0], 1024), BF16), pltpu.VMEM((block, cols), F32),
+    pl.run_scoped(attend, pltpu.VMEM((2, wo_ref.shape[0] // groups, model), BF16), pltpu.VMEM((rows, model), F32), pltpu.VMEM((block, cols), F32),
                   pltpu.VMEM((block, cols), F32), pltpu.VMEM((2 * n_tiles, hd, cols), BF16),
                   pltpu.VMEM((2 * n_tiles, 1, cols), F32), pltpu.VMEM((2 * n_tiles, 1, cols), F32),
                   pltpu.VMEM((2 * n_tiles, hd, cols), F32))
@@ -393,9 +407,10 @@
         return pl.pallas_call(
             functools.partial(layer_kernel, n_outer, n_inner),
             out_shape=jax.ShapeDtypeStruct((rows, model), BF16),
-            in_specs=[vmem] * 3 + [hbm] * 4,
+            in_specs=[hbm] + [vmem] * 2 + [hbm] * 4,
             out_specs=vmem,
             scratch_shapes=[
+                pltpu.VMEM((rows, model), BF16),
                 pltpu.VMEM((2, n_inner + q_heads, chunk, hd), BF16),
                 pltpu.VMEM((2, n_inner, hd, chunk), BF16),
                 pltpu.VMEM((2 * n_outer, block, hd), BF16),
@@ -403,9 +418,9 @@
                 pltpu.VMEM((2, per_kv, block, hd), BF16),
                 pltpu.VMEM((2, n_tiles, 2 * chunk, per_kv * hd), BF16),
                 pltpu.VMEM((rows, q_heads * hd), BF16),
-                dma((2,)), pair, pair, pair, pair, pair, pair, pair, pair, dma((3, 4)), dma((3, 4)),
+                dma((3,)), pair, pair, pair, pair, pair, pair, pair, pair, dma((3, 4)), dma((3, 4)),
             ],
-            compiler_params=pltpu.CompilerParams(collective_id=0, has_side_effects=True, vmem_limit_bytes=56 * 1024 * 1024),
+            compiler_params=pltpu.CompilerParams(collective_id=0, has_side_effects=True, vmem_limit_bytes=62 * 1024 * 1024),
         )(hidden, cos, sin, w_query, w_key, w_value, w_out.reshape(q_heads * hd, model))
 
     row_spec = P(('dp', 'cpo', 'cpi'), None)

time: 109 us -> 103 us (0.945)
  Pallas kernels: 104 us -> 97.9 us
    pallas_call x1, Pallas kernels: 104 us -> 97.9 us  [device_step(): pl.pallas_call(functools.partial(layer_kernel, n_outer, n_inner), out_sha...]
where the time goes in v3:
time: 103 us; the launch traced here: 102 us
  Pallas kernels  97.9 us (95%)
  local copies, waits for them, and re-layouts  3.13 us (3%)
  other arithmetic  1.28 us (1%)
    pallas_call x1, Pallas kernels, device_step(): pl.pallas_call(functools.partial(layer_kernel, n_outer, n_inner), out_sha...  97.9 us
    unnamed x1, local copies, waits for them, and re-layouts  3.13 us

profile of v3, /device:TPU:97, one launch (start us, length us, event | category | flops | bytes accessed | tf_op | source)
XLA Modules:
  0.0 102.3 jit_solution(15716886324899051347)
XLA Ops:
  0.0 1.2 %negate_select_fusion = (f32[256,128]{1,0:T(8,128)}, f32[256,128]{1,0:T(8,128)}) fusion(f32[128]{0:T(128)S(1)} %fusion.2, f32[256]{0:T(256)S(1)} %add_convert_fusion, pred[128]{0:T(512)(128)(4,1)S(1)} %iota_compare_fusion), kind=kLoop, calls=%fused_computation | loop fusion | flops 98304 | bytes 263808 | tf_op jit(solution)/shard_map/jit(_where)/select_n | solution.py:23
  1.3 97.9 %shard_map.55 = bf16[256,4096]{1,0:T(8,128)(2,1)} custom-call(bf16[256,4096]{1,0:T(8,128)(2,1)} %x_hbm.1, f32[256,128]{1,0:T(8,128)} %get-tuple-element.6.cos_ref, f32[256,128]{1,0:T(8,128)} %get-tuple-element.5.sin_ref, bf16[4096,32,128]{2,1,0:T(8,128)(2,1)} %wq_ref.1, bf16[4096,8,128]{2,1,0:T(8,128)(2,1)} %wk_ref.1, bf16[4096,8,128]{2,1,0:T(8,128)(2,1)} %wv_ref.1, ...), custom_call_target="tpu_custom_call" | custom-call | tf_op jit(solution)/shard_map/pallas_call | solution.py:407
  99.2 3.1 %copy.7 = bf16[256,4096]{1,0:T(8,128)(2,1)} copy(bf16[256,4096]{1,0:T(8,128)(2,1)} %shard_map.55) | data formatting | bytes 4194304
  (4 shorter events, 0.0 us)
